TPU v7x, 32 devices: a whole 2x2x4 slice. The times are simulated.
32 devices in a mesh: field: 8 (over z, x), dom: 4 (over y, core).
Axes of the slice: x: 2, y: 2, z: 4, core: 2. Of those that a mesh axis runs over, the one named last changes fastest.
Arguments:
- coefficients: float32 [256, 128], P('dom'), may hold values from -6 to 6
- copies: int32 [256], P('dom'), may hold values from 1 to 4
- owner: int32 [256, 1], P('dom'), may hold values from 0 to 3; in each aligned block of 64 rows (0 to 63, 64 to 127, ...) at most 32 rows name the same one
- snapshots: int32 [8], replicated, may hold values from 0 to 255
- basis: bfloat16 [4194304, 128], P(('field', 'dom')), may hold values from -3 to 3
- observed: float32 [4194304], P(('field', 'dom')), may hold values from -6 to 6
- precision: float32 [4194304], P(('field', 'dom')), may hold values from 1 to 16
Outputs:
- new_coefficients: float32 [4, 4, 32, 128], P('dom')
Inputs may be any that keep to these rules, and one draw needn't show every extreme that they name: Among the 64 particles of one index of dom, at most 32 name the same owner, and in every draw some owner is named by exactly 32 particles of some index of dom.
All inputs are finite; a program needn't handle non-finite values.
Results may differ from a plain program's by a relative error of at most 0.00074.
Values sent between devices are 32-bit elements; how exact they have to be, the bound alone decides.
A program may use at most 192 MiB of HBM per device.

v0:
```python
import functools
import math

import jax
import jax.numpy as jnp
from jax import lax
from jax.experimental import pallas as pl
from jax.experimental.pallas import tpu as pltpu
from jax.sharding import PartitionSpec as P

highest = lax.Precision.HIGHEST
last_pair = (((1,), (1,)), ((), ()))


def pack_rows(updated, owner_column, slot_count, owners):
    labels = owner_column[:, 0]
    onehot = (labels[:, None] == jnp.arange(owners, dtype=jnp.int32)[None, :]).astype(jnp.int32)
    before = jnp.sum(onehot * (jnp.cumsum(onehot, axis=0) - 1), axis=1)
    target = labels * slot_count + before
    placing = (jnp.arange(owners * slot_count, dtype=jnp.int32)[:, None] == target[None, :]).astype(
        jnp.int32
    )
    source = jnp.sum(placing * jnp.arange(updated.shape[0], dtype=jnp.int32)[None, :], axis=1)
    filled = jnp.sum(placing, axis=1) > 0
    packed = jnp.where(filled[:, None], updated[source], jnp.zeros((), jnp.float32))
    return packed.reshape(owners, slot_count, updated.shape[1])


def local_kernel(density, snaps, coef_ref, basis_ref, obs_ref, prec_ref, out_ref, lhs_ref):
    rows = coef_ref.shape[0]
    particles = rows - 16
    rank = basis_ref.shape[1]

    @pl.when(pl.program_id(0) == 0)
    def _():
        out_ref[...] = jnp.zeros_like(out_ref)

    basis = basis_ref[...]
    observed = obs_ref[...]
    weight = density * prec_ref[...]
    field = lax.dot_general(coef_ref[...], basis, last_pair, preferred_element_type=jnp.float32)
    slopes = jnp.tanh(field - observed)
    lhs_ref[:particles, :] = (weight * slopes[:particles]).astype(jnp.bfloat16)
    tail = slopes[particles:particles + snaps]
    bend = weight * (1.0 - tail * tail)
    turned = basis.T
    for s in range(snaps):
        row = bend[s:s + 1].astype(jnp.bfloat16)
        lhs_ref[particles + s * rank:particles + (s + 1) * rank, :] = row * turned
    out_ref[...] += jnp.dot(lhs_ref[...], basis, preferred_element_type=jnp.float32)


def local_sums(density, rounded, picked, basis, observed, precision, tile):
    points, rank = basis.shape
    particles, snaps = rounded.shape[0], picked.shape[0]
    tile = math.gcd(points, tile)
    spare = jnp.zeros((16 - snaps, rank), jnp.bfloat16)
    stacked = jnp.concatenate([rounded, picked, spare], axis=0)
    total = particles + snaps * rank
    return pl.pallas_call(
        functools.partial(local_kernel, density, snaps),
        grid=(points // tile,),
        in_specs=[
            pl.BlockSpec((particles + 16, rank), lambda i: (0, 0)),
            pl.BlockSpec((tile, rank), lambda i: (i, 0)),
            pl.BlockSpec((1, tile), lambda i: (0, i)),
            pl.BlockSpec((1, tile), lambda i: (0, i)),
        ],
        out_specs=pl.BlockSpec((total, rank), lambda i: (0, 0)),
        out_shape=jax.ShapeDtypeStruct((total, rank), jnp.float32),
        scratch_shapes=[pltpu.VMEM((total, tile), jnp.bfloat16)],
        compiler_params=pltpu.CompilerParams(
            dimension_semantics=("arbitrary",), vmem_limit_bytes=56 * 1024 * 1024
        ),
    )(stacked, basis, observed.reshape(1, points), precision.reshape(1, points))


def body(coefficients, copies, owner, snapshots, basis, observed, precision):
    owners = lax.axis_size("dom")
    block_rows = coefficients.shape[0]
    rank_width = coefficients.shape[1]
    points = basis.shape[0] * lax.axis_size("field") * owners
    density = rank_width / points
    everyone, counts = (
        lax.all_gather(coefficients, "dom", axis=0, tiled=True),
        lax.all_gather(copies.astype(jnp.float32), "dom", axis=0, tiled=True),
    )
    rounded = everyone.astype(jnp.bfloat16)
    total_rows = everyone.shape[0]
    picked = rounded[snapshots]
    snaps = snapshots.shape[0]
    sums = local_sums(density, rounded, picked, basis, observed, precision, 2048)
    sums = lax.psum(sums, ("field", "dom"))
    grad_sum = sums[:total_rows]
    hess_sum = sums[total_rows:].reshape(snaps, rank_width, rank_width)
    hessians = jnp.eye(rank_width, dtype=jnp.float32)[None] + hess_sum
    mean_hess = jnp.mean(hessians, axis=0)
    hess_trace = jnp.trace(mean_hess)
    repulse = 6.0 / hess_trace
    lifted = jnp.dot(everyone, mean_hess, precision=highest)
    quad_norms = jnp.sum(lifted * everyone, axis=1)
    carried_low = (everyone + repulse * lifted).astype(jnp.bfloat16)
    block_first = lax.axis_index("dom") * block_rows
    row_count = block_rows // lax.axis_size("field")
    row_start = block_first + lax.axis_index("field") * row_count
    own_lift = lax.dynamic_slice_in_dim(lifted, row_start, row_count, 0)
    own_norms = lax.dynamic_slice_in_dim(quad_norms, row_start, row_count, 0)
    cross_terms = lax.dot_general(
        own_lift, everyone, last_pair, precision=highest, preferred_element_type=jnp.float32
    )
    distance = own_norms[:, None] + quad_norms[None, :] - 2.0 * cross_terms
    weights = counts[None, :] * jnp.exp(-3.0 * distance / hess_trace)
    weight_total = jnp.sum(weights, axis=1)
    weights_low = weights.astype(jnp.bfloat16)
    numerator = jnp.dot(weights_low, carried_low, preferred_element_type=jnp.float32)
    numerator = numerator + jnp.dot(weights_low.astype(jnp.float32), grad_sum, precision=highest)
    drift_rows = -numerator / weight_total[:, None] + repulse * own_lift
    snap_coef = everyone[snapshots]
    snap_cross = lax.dot_general(
        own_lift, snap_coef, last_pair, precision=highest, preferred_element_type=jnp.float32
    )
    snap_dist = own_norms[:, None] + quad_norms[snapshots][None, :] - 2.0 * snap_cross
    mixture = 1.0 / jnp.square(1.0 + snap_dist / hess_trace)
    mixture = mixture / jnp.sum(mixture, axis=1, keepdims=True)
    local_hess = jnp.einsum("is,srq->irq", mixture, hessians, precision=highest)
    factor = jnp.linalg.cholesky(local_hess)
    halfway = jax.scipy.linalg.solve_triangular(factor, drift_rows[:, :, None], lower=True)
    newton_step = jax.scipy.linalg.solve_triangular(factor, halfway, lower=True, trans=1)
    updated = lax.dynamic_slice_in_dim(everyone, row_start, row_count, 0) + newton_step[:, :, 0]
    updated = lax.all_gather(updated, "field", axis=0, tiled=True)
    packed = pack_rows(updated, owner, 2 * block_rows // owners, owners)
    arrived = lax.all_to_all(packed, "dom", split_axis=0, concat_axis=0, tiled=True)
    return arrived[None]


def solution(mesh):
    return jax.shard_map(
        body,
        mesh=mesh,
        in_specs=(
            P("dom", None),
            P("dom"),
            P("dom", None),
            P(),
            P(("field", "dom"), None),
            P(("field", "dom")),
            P(("field", "dom")),
        ),
        out_specs=P("dom", None, None, None),
        check_vma=False,
    )
```

profile of v0, /device:TPU:0, one launch (start us, length us, event | category | flops | bytes accessed | tf_op | source)
XLA Modules:
  0.0 495.8 jit_solution(7173215884951871130)
XLA Ops:
  6.5 6.9 %all_gather.9 = f32[256,128]{1,0:T(8,128)S(1)} all-gather(f32[64,128]{1,0:T(8,128)} %param.7), channel_id=1, replica_groups=mesh['field'=8,'dom'=4] {'dom'}, dimensions={0}, use_global_device_ids=true | all-gather | bytes 163840 | tf_op jit(solution)/shard_map/all_gather | solution.py:85
  13.4 0.7 compare_select_fusion.1
  14.1 0.6 gather_fusion
  14.8 0.7 maximum_maximum_fusion.coef_ref
  15.5 121.1 %shard_map.73 = f32[1280,128]{1,0:T(8,128)} custom-call(bf16[272,128]{1,0:T(8,128)(2,1)} %maximum_maximum_fusion.coef_ref, bf16[131072,128]{1,0:T(8,128)(2,1)} %basis_ref.1, f32[1,131072]{1,0:T(1,128)} %bitcast.58, f32[1,131072]{1,0:T(1,128)} %bitcast.59), custom_call_target="tpu_custom_call" | custom-call | tf_op jit(solution)/shard_map/pallas_call | solution.py:60
  136.6 0.6 gather_fusion.2
  137.2 0.6 dynamic-slice.1
  138.5 7.8 %all-reduce = f32[256]{0:T(256)S(1)} all-reduce(f32[256]{0:T(256)S(1)} %convert_dynamic-update-slice_fusion), channel_id=1, replica_groups=mesh['field'=8,'dom'=4] {'dom'}, use_global_device_ids=true, to_apply=%add | all-reduce | flops 256 | bytes 2048
  147.0 121.0 %all-reduce.3.cloned.1.call-done = f32[1280,128]{1,0:T(8,128)} async-done(((f32[1280,128]{1,0:T(8,128)}), f32[1280,128]{1,0:T(8,128)}) %all-reduce.3.cloned.1.call-update) | async-done | bytes 655376 | tf_op jit(solution)/shard_map/psum | solution.py:93
  267.9 1.1 slice.34
  269.8 0.6 select_reduce_fusion.1
  270.5 0.6 gather_fusion.1
  271.9 1.0 fusion.45
  272.9 0.8 divide_reduce_fusion
  273.7 0.8 fusion.16
  274.9 93.8 %custom-call.11 = f32[8,128,128]{2,1,0:T(8,128)S(1)} custom-call(f32[8,128,128]{2,1,0:T(8,128)S(1)} %fusion.15), custom_call_target="Cholesky" | custom-call | tf_op jit(solution)/shard_map/jit(cholesky)/cholesky | solution.py:126
  369.0 78.6 %custom-call.12 = f32[8,1,128,128]{2,3,1,0:T(8,128)S(1)} custom-call(f32[8,1,128,128]{3,2,1,0:T(8,128)S(1)} %select_bitcast_fusion), custom_call_target="InvertDiagBlocksLowerTriangular" | custom-call | tf_op jit(solution)/shard_map/jit(_solve_triangular)/vmap()/triangular_solve | solution.py:128
  447.7 1.1 fusion.7
  448.8 0.6 convolution_bitcast_fusion
  449.4 0.9 fusion.12
  450.3 30.6 %all_gather.11 = f32[64,128]{1,0:T(8,128)S(1)} all-gather(f32[8,128]{1,0:T(8,128)S(1)} %dynamic-slice_add_fusion), channel_id=1, replica_groups=mesh['field'=8,'dom'=4] {'field'}, dimensions={0}, use_global_device_ids=true | all-gather | bytes 36864 | tf_op jit(solution)/shard_map/all_gather | solution.py:130
  480.9 0.6 gather_fusion.3
  481.6 6.7 %all_to_all.5 = f32[4,32,128]{2,1,0:T(8,128)S(1)} all-to-all(f32[4,32,128]{2,1,0:T(8,128)S(1)} %broadcast_select_fusion), channel_id=1, replica_groups=mesh['field'=8,'dom'=4] {'dom'}, dimensions={0} | all-to-all | bytes 131072 | tf_op jit(solution)/shard_map/all_to_all | solution.py:132
  488.3 0.6 copy.46
  (37 shorter events, 2.6 us)
Async XLA Ops:
  6.5 130.6 %copy-start.2 = (u32[32]{0:T(128)S(1)}, u32[32]{0:T(128)}, u32[]{:S(2)}) copy-start(u32[32]{0:T(128)} %constant.103) | copy-start | bytes 388
  6.5 131.9 %copy-start.1 = (s32[64]{0:T(128)S(1)}, s32[64]{0:T(128)}, u32[]{:S(2)}) copy-start(s32[64]{0:T(128)} %param.8) | copy-start | bytes 772
  6.5 139.8 %copy-start = (s32[64,1]{0,1:T(1,128)S(1)}, s32[64,1]{0,1:T(1,128)}, u32[]{:S(2)}) copy-start(s32[64,1]{0,1:T(1,128)} %param.9) | copy-start | bytes 772
  6.5 261.4 %all-reduce.3.cloned.1.call-start = ((), (), s32[]{:S(2)}) async-start(), calls=%async_computation.1 | async-start | bytes 1310720 | tf_op jit(solution)/shard_map/psum | solution.py:93
Sparse Core Ops, SparseCore 0:
  136.7 131.2 all-reduce.2
where the time goes:
time: 496 us
  other arithmetic  176 us (35%)
  Pallas kernels  121 us (24%)
  waiting for transfers between devices  121 us (24%)
  blocking collectives  52 us (10%)
  between operations  14.9 us (3%)
  matrix products  5.68 us (1%)
  local copies, waits for them, and re-layouts  5.17 us (1%)
    pallas_call x1, Pallas kernels, local_sums(): pl.pallas_call(functools.partial(local_kernel, density, snaps), grid=(poi...  121 us
    psum x1, waiting for transfers between devices, body(): sums = lax.psum(sums, ('field', 'dom'))  121 us
    another operation x4, other arithmetic, body(): factor = jnp.linalg.cholesky(local_hess)  94 us
    another operation x3, other arithmetic, body(): jax.scipy.linalg.solve_triangular(factor, halfway, lower=True, trans=1)  78.7 us
    all_gather x1, blocking collectives, body(): updated = lax.all_gather(updated, 'field', axis=0, tiled=True)  30.6 us
  transfers between devices with their start and end apart: 1, of which 1 were waited for; matrix products, arithmetic and copies ran while one was open for 0% of the time, Pallas kernels for 0%

commit v1 on v0

v1 whole, which is shorter than its diff:
```python
import functools
import math

import jax
import jax.numpy as jnp
from jax import lax
from jax.experimental import pallas as pl
from jax.experimental.pallas import tpu as pltpu
from jax.sharding import PartitionSpec as P

highest = lax.Precision.HIGHEST
last_pair = (((1,), (1,)), ((), ()))
MESH = pl.DeviceIdType.MESH
VMEM = pltpu.MemorySpace.VMEM
GROUP = 8


def round_up(value, unit):
    return -(-value // unit) * unit


def gather_kernel(dom_size, msg_ref, out_ref, send_sem, recv_sem, local_sem):
    me = lax.axis_index("dom")
    barrier = pltpu.get_barrier_semaphore()
    for step in range(1, dom_size):
        peer = lax.rem(me + step, dom_size)
        pl.semaphore_signal(barrier, inc=1, device_id={"dom": peer}, device_id_type=MESH)
    own = pltpu.make_async_copy(msg_ref, out_ref.at[me], local_sem)
    own.start()
    pl.semaphore_wait(barrier, dom_size - 1)
    copies = []
    for step in range(1, dom_size):
        peer = lax.rem(me + step, dom_size)
        copy = pltpu.make_async_remote_copy(
            src_ref=msg_ref,
            dst_ref=out_ref.at[me],
            send_sem=send_sem.at[step - 1],
            recv_sem=recv_sem.at[step - 1],
            device_id={"dom": peer},
            device_id_type=MESH,
        )
        copy.start()
        copies.append(copy)
    own.wait()
    for copy in copies:
        copy.wait()


def gather_dom(msg):
    dom_size = lax.axis_size("dom")
    return pl.pallas_call(
        functools.partial(gather_kernel, dom_size),
        out_shape=jax.ShapeDtypeStruct((dom_size,) + msg.shape, msg.dtype),
        in_specs=[pl.BlockSpec(memory_space=VMEM)],
        out_specs=pl.BlockSpec(memory_space=VMEM),
        scratch_shapes=[
            pltpu.SemaphoreType.DMA((dom_size - 1,)),
            pltpu.SemaphoreType.DMA((dom_size - 1,)),
            pltpu.SemaphoreType.DMA,
        ],
        compiler_params=pltpu.CompilerParams(collective_id=0, has_side_effects=True),
    )(msg)


def local_kernel(density, snaps, coef_ref, basis_ref, obs_ref, prec_ref, out_ref, lhs_ref):
    rows = coef_ref.shape[0]
    particles = rows - 16
    rank = basis_ref.shape[1]
    total = particles + snaps * rank

    @pl.when(pl.program_id(0) == 0)
    def _():
        out_ref[...] = jnp.zeros_like(out_ref)

    basis = basis_ref[...]
    observed = obs_ref[...]
    weight = density * prec_ref[...]
    field = lax.dot_general(coef_ref[...], basis, last_pair, preferred_element_type=jnp.float32)
    slopes = jnp.tanh(field - observed)
    lhs_ref[:particles, :] = (weight * slopes[:particles]).astype(jnp.bfloat16)
    tail = slopes[particles:particles + snaps]
    bend = weight * (1.0 - tail * tail)
    turned = basis.T
    for s in range(snaps):
        row = bend[s:s + 1].astype(jnp.bfloat16)
        lhs_ref[particles + s * rank:particles + (s + 1) * rank, :] = row * turned
    out_ref[:total] += jnp.dot(lhs_ref[...], basis, preferred_element_type=jnp.float32)


def local_sums(density, stacked, snaps, basis, observed, precision, tile, padded):
    points, rank = basis.shape
    particles = stacked.shape[0] - 16
    tile = math.gcd(points, tile)
    total = particles + snaps * rank
    return pl.pallas_call(
        functools.partial(local_kernel, density, snaps),
        grid=(points // tile,),
        in_specs=[
            pl.BlockSpec((particles + 16, rank), lambda i: (0, 0)),
            pl.BlockSpec((tile, rank), lambda i: (i, 0)),
            pl.BlockSpec((1, tile), lambda i: (0, i)),
            pl.BlockSpec((1, tile), lambda i: (0, i)),
        ],
        out_specs=pl.BlockSpec((padded, rank), lambda i: (0, 0)),
        out_shape=jax.ShapeDtypeStruct((padded, rank), jnp.float32),
        scratch_shapes=[pltpu.VMEM((total, tile), jnp.bfloat16)],
        compiler_params=pltpu.CompilerParams(
            dimension_semantics=("arbitrary",), vmem_limit_bytes=56 * 1024 * 1024
        ),
    )(stacked, basis, observed.reshape(1, points), precision.reshape(1, points))


def reduce_kernel(half_dom, peers, part_ref, out_ref, pair_ref, held_ref, land_ref,
                  pair_send, pair_recv, give_send, give_recv, back_send, back_recv,
                  pass_send, pass_recv):
    dom = lax.axis_index("dom")
    field = lax.axis_index("field")
    core = lax.rem(dom, 2)
    other = dom + 1 - 2 * core
    me = field * half_dom + dom // 2

    def place(peer):
        return (peer // half_dom, lax.rem(peer, half_dom) * 2 + core)

    barrier = pltpu.get_barrier_semaphore()

    def greet(step, carry):
        pl.semaphore_signal(
            barrier, inc=1, device_id=place(lax.rem(me + step, peers)), device_id_type=MESH
        )
        return carry

    pl.semaphore_signal(barrier, inc=1, device_id=(field, other), device_id_type=MESH)
    lax.fori_loop(1, peers, greet, 0)
    pl.semaphore_wait(barrier, peers)

    def pair_copy(peer):
        return pltpu.make_async_remote_copy(
            src_ref=part_ref.at[1 - core, peer],
            dst_ref=pair_ref.at[peer],
            send_sem=pair_send.at[peer],
            recv_sem=pair_recv.at[peer],
            device_id=(field, other),
            device_id_type=MESH,
        )

    def give_copy(step):
        peer = lax.rem(me + step, peers)
        return pltpu.make_async_remote_copy(
            src_ref=held_ref.at[peer],
            dst_ref=land_ref.at[step],
            send_sem=give_send.at[step],
            recv_sem=give_recv.at[step],
            device_id=place(peer),
            device_id_type=MESH,
        )

    def back_copy(step):
        return pltpu.make_async_remote_copy(
            src_ref=out_ref.at[core, me],
            dst_ref=out_ref.at[core, me],
            send_sem=back_send.at[step],
            recv_sem=back_recv.at[step],
            device_id=place(lax.rem(me + step, peers)),
            device_id_type=MESH,
        )

    def pass_copy(step):
        peer = lax.rem(me + peers - step, peers)
        return pltpu.make_async_remote_copy(
            src_ref=out_ref.at[core, peer],
            dst_ref=out_ref.at[core, peer],
            send_sem=pass_send.at[step],
            recv_sem=pass_recv.at[step],
            device_id=(field, other),
            device_id_type=MESH,
        )

    def start_pair(step, carry):
        pair_copy(lax.rem(me + step, peers)).start()
        return carry

    lax.fori_loop(1, peers + 1, start_pair, 0)

    def combine(step, carry):
        peer = lax.rem(me + step, peers)
        pair_copy(peer).wait_recv()
        held_ref[peer] = part_ref[core, peer] + pair_ref[peer]

        @pl.when(step < peers)
        def _():
            give_copy(step).start()

        return carry

    lax.fori_loop(1, peers + 1, combine, 0)

    def absorb(step, total):
        give_copy(step).wait_recv()
        return total + land_ref[step]

    out_ref[core, me] = lax.fori_loop(1, peers, absorb, held_ref[me])

    def start_back(step, carry):
        back_copy(step).start()
        return carry

    lax.fori_loop(1, peers, start_back, 0)
    pass_copy(0).start()

    def forward(step, carry):
        back_copy(step).wait_recv()
        pass_copy(step).start()
        return carry

    lax.fori_loop(1, peers, forward, 0)

    def drain(step, carry):
        pass_copy(step).wait_recv()
        pass_copy(step).wait_send()
        pair_copy(step).wait_send()
        return carry

    lax.fori_loop(0, peers, drain, 0)

    def drain_sends(step, carry):
        give_copy(step).wait_send()
        back_copy(step).wait_send()
        return carry

    lax.fori_loop(1, peers, drain_sends, 0)


def reduce_all(part):
    half_dom = lax.axis_size("dom") // 2
    peers = lax.axis_size("field") * half_dom
    rank = part.shape[1]
    piece = part.shape[0] // (2 * peers)
    dma = pltpu.SemaphoreType.DMA
    total = pl.pallas_call(
        functools.partial(reduce_kernel, half_dom, peers),
        out_shape=jax.ShapeDtypeStruct((2, peers, piece, rank), part.dtype),
        in_specs=[pl.BlockSpec(memory_space=VMEM)],
        out_specs=pl.BlockSpec(memory_space=VMEM),
        scratch_shapes=[pltpu.VMEM((peers, piece, rank), part.dtype)] * 3 + [dma((peers,))] * 8,
        compiler_params=pltpu.CompilerParams(collective_id=1, has_side_effects=True),
    )(part.reshape(2, peers, piece, rank))
    return total.reshape(part.shape)


def lane_of(row, lane):
    return jnp.broadcast_to(row[:, lane:lane + 1], row.shape)


def newton_kernel(snaps, total_ref, everyone_ref, counts_ref, own_ref, snap_ref, out_ref,
                  grid_ref):
    particles, rank = everyone_ref.shape
    height = own_ref.shape[0]
    f32 = jnp.float32
    dot = functools.partial(jnp.dot, precision=highest, preferred_element_type=f32)
    turned_dot = functools.partial(
        lax.dot_general, dimension_numbers=last_pair, precision=highest, preferred_element_type=f32
    )
    diagonal = (
        lax.broadcasted_iota(jnp.int32, (rank, rank), 0)
        == lax.broadcasted_iota(jnp.int32, (rank, rank), 1)
    )

    def hess(s):
        return total_ref[particles + s * rank:particles + (s + 1) * rank, :]

    mean = hess(0)
    for s in range(1, snaps):
        mean = mean + hess(s)
    mean = mean * (1.0 / snaps) + jnp.where(diagonal, 1.0, 0.0)
    trace = jnp.sum(jnp.sum(jnp.where(diagonal, mean, 0.0), axis=1, keepdims=True), axis=0, keepdims=True)
    repulse = 6.0 / trace
    everyone = everyone_ref[...]
    own = own_ref[...]
    snap = snap_ref[...]
    ones = jnp.ones((8, rank), f32)
    lifted = dot(everyone, mean)
    own_lift = dot(own, mean)
    snap_lift = dot(snap, mean)
    quad_row = turned_dot(ones, lifted * everyone)[:1]
    snap_row = turned_dot(ones, snap_lift * snap)[:1]
    own_quad = jnp.sum(own_lift * own, axis=1, keepdims=True)
    distance = own_quad + quad_row - 2.0 * turned_dot(own_lift, everyone)
    weights = counts_ref[...] * jnp.exp(-3.0 * distance / trace)
    weight_total = jnp.sum(weights, axis=1, keepdims=True)
    weights_low = weights.astype(jnp.bfloat16)
    carried_low = (everyone + repulse * lifted).astype(jnp.bfloat16)
    numerator = jnp.dot(weights_low, carried_low, preferred_element_type=f32)
    numerator = numerator + dot(weights_low.astype(f32), total_ref[:particles, :])
    drift = -numerator / weight_total + repulse * own_lift
    snap_dist = own_quad + snap_row - 2.0 * turned_dot(own_lift, snap)
    shifted = 1.0 + snap_dist / trace
    mixture = 1.0 / (shifted * shifted)
    mixture = mixture / jnp.sum(mixture, axis=1, keepdims=True)

    shares = [jnp.broadcast_to(mixture[:, s:s + 1], (height, rank)) for s in range(snaps)]
    lanes = lax.broadcasted_iota(jnp.int32, (height, rank), 1)

    def blend(block, carry):
        first = pl.multiple_of(block * 8, 8)
        groups = [total_ref[pl.ds(particles + s * rank + first, 8), :] for s in range(snaps)]
        for r in range(8):
            line = jnp.where(lanes == first + r, 1.0, 0.0)
            for s in range(snaps):
                line = line + shares[s] * groups[s][r:r + 1, :]
            grid_ref[first + r] = line
        return carry

    lax.fori_loop(0, rank // 8, blend, 0)

    state = drift
    for first in range(0, rank, GROUP):
        rows = [grid_ref[first + a] for a in range(GROUP)]
        corner = [[lane_of(rows[a], first + c) if c >= a else None for c in range(GROUP)] for a in range(GROUP)]
        inverse, factors = [], {}
        for a in range(GROUP):
            inverse.append(1.0 / corner[a][a])
            for c in range(a + 1, GROUP):
                factors[a, c] = corner[a][c] * inverse[a]
            for c in range(a + 1, GROUP):
                for e in range(c, GROUP):
                    corner[c][e] = corner[c][e] - factors[a, c] * corner[a][e]
        wiped = []
        for a in range(GROUP):
            line = rows[a]
            for c in range(a):
                line = jnp.where(lanes == first + c, 0.0, line) - factors[c, a] * wiped[c]
            wiped.append(jnp.where(lanes == first + a, 1.0, line))
        inside = (lanes >= first) & (lanes < first + GROUP)
        below = [jnp.where(inside & (lanes > first + a), 0.0, wiped[a]) for a in range(GROUP)]
        scaled = [wiped[a] * inverse[a] for a in range(GROUP)]
        for j in range(first + GROUP, rank):
            line = jnp.where(inside, 0.0, grid_ref[j])
            for a in range(GROUP):
                line = line - lane_of(scaled[a], j) * below[a]
            grid_ref[j] = line
        heads = [lane_of(state, first + a) for a in range(GROUP)]
        for a in range(GROUP):
            for c in range(a + 1, GROUP):
                heads[c] = heads[c] - factors[a, c] * heads[a]
        state = jnp.where(inside, 0.0, state)
        for a in range(GROUP):
            state = state - (heads[a] * inverse[a]) * below[a]
    out_ref[...] = own - state


def newton_rows(snaps, total, everyone, counts, own, snap):
    rank = everyone.shape[1]
    height = own.shape[0]
    return pl.pallas_call(
        functools.partial(newton_kernel, snaps),
        out_shape=jax.ShapeDtypeStruct((height, rank), jnp.float32),
        in_specs=[pl.BlockSpec(memory_space=VMEM)] * 5,
        out_specs=pl.BlockSpec(memory_space=VMEM),
        scratch_shapes=[pltpu.VMEM((rank, height, rank), jnp.float32)],
        compiler_params=pltpu.CompilerParams(vmem_limit_bytes=32 * 1024 * 1024),
    )(total, everyone, counts, own, snap)


def place_kernel(field_size, peers, slots, moved_ref, owner_ref, out_ref, all_ref, send_sem, recv_sem):
    dom = lax.axis_index("dom")
    me = dom * field_size + lax.axis_index("field")
    height = moved_ref.shape[0]
    columns = owner_ref.shape[1]
    spread = out_ref.shape[0]
    barrier = pltpu.get_barrier_semaphore()

    def spot(step):
        peer = lax.rem(me + step, peers)
        return (lax.rem(peer, field_size), peer // field_size)

    def greet(step, carry):
        pl.semaphore_signal(barrier, inc=1, device_id=spot(step), device_id_type=MESH)
        return carry

    def copy_to(step):
        return pltpu.make_async_remote_copy(
            src_ref=moved_ref,
            dst_ref=all_ref.at[me],
            send_sem=send_sem.at[step],
            recv_sem=recv_sem.at[step],
            device_id=spot(step),
            device_id_type=MESH,
        )

    def start(step, carry):
        copy_to(step).start()
        return carry

    def finish(step, carry):
        copy_to(step).wait()
        return carry

    lax.fori_loop(1, peers, greet, 0)
    pl.semaphore_wait(barrier, peers - 1)
    lax.fori_loop(1, peers, start, 0)
    all_ref[me] = moved_ref[...]
    mine = owner_ref[...] == dom.astype(jnp.float32)
    group = field_size * height
    row = lax.broadcasted_iota(jnp.int32, (columns, columns), 0)
    col = lax.broadcasted_iota(jnp.int32, (columns, columns), 1)
    earlier = jnp.where((row < col) & (row // group == col // group), 1.0, 0.0).astype(jnp.bfloat16)
    flags = jnp.broadcast_to(jnp.where(mine, 1.0, 0.0), (8, columns)).astype(jnp.bfloat16)
    before = jnp.dot(flags, earlier, preferred_element_type=jnp.float32)[:1]
    base = (lax.broadcasted_iota(jnp.int32, (1, columns), 1) // group * slots).astype(jnp.float32)
    target = jnp.where(mine, base + before, -1.0)
    lines = lax.broadcasted_iota(jnp.int32, (spread, columns), 0).astype(jnp.float32)
    placing = jnp.where(lines == target, 1.0, 0.0)
    lax.fori_loop(1, peers, finish, 0)
    moved = all_ref[...].reshape(columns, all_ref.shape[2])
    out_ref[...] = jnp.dot(placing, moved, precision=highest, preferred_element_type=jnp.float32)


def place_rows(moved, owners, slots):
    field_size, dom_size = lax.axis_size("field"), lax.axis_size("dom")
    peers = field_size * dom_size
    height, rank = moved.shape
    return pl.pallas_call(
        functools.partial(place_kernel, field_size, peers, slots),
        out_shape=jax.ShapeDtypeStruct((dom_size * slots, rank), jnp.float32),
        in_specs=[pl.BlockSpec(memory_space=VMEM)] * 2,
        out_specs=pl.BlockSpec(memory_space=VMEM),
        scratch_shapes=[
            pltpu.VMEM((peers, height, rank), jnp.float32),
            pltpu.SemaphoreType.DMA((peers,)),
            pltpu.SemaphoreType.DMA((peers,)),
        ],
        compiler_params=pltpu.CompilerParams(collective_id=2, has_side_effects=True),
    )(moved, owners)


def body(coefficients, copies, owner, snapshots, basis, observed, precision):
    dom_size, field_size = lax.axis_size("dom"), lax.axis_size("field")
    devices = dom_size * field_size
    block_rows, rank = coefficients.shape
    points = basis.shape[0] * devices
    density = rank / points
    snaps = snapshots.shape[0]
    labels = jnp.stack([copies.astype(jnp.float32), owner[:, 0].astype(jnp.float32)])
    labels = jnp.pad(labels, ((0, 6), (0, rank - block_rows)))
    gathered = gather_dom(jnp.concatenate([coefficients, labels], axis=0))
    everyone = gathered[:, :block_rows].reshape(dom_size * block_rows, rank)
    counts = gathered[:, block_rows, :block_rows].reshape(1, dom_size * block_rows)
    owners = gathered[:, block_rows + 1, :block_rows]
    particles = everyone.shape[0]
    snap_coef = everyone[snapshots]
    spare = jnp.zeros((16 - snaps, rank), jnp.float32)
    stacked = jnp.concatenate([everyone, snap_coef, spare], axis=0).astype(jnp.bfloat16)
    padded = round_up(-(-(particles + snaps * rank) // devices), 8) * devices
    part = local_sums(density, stacked, snaps, basis, observed, precision, 2048, padded)
    total = reduce_all(part)
    row_count = block_rows // field_size
    height = round_up(row_count, 8)
    own = lax.dynamic_slice_in_dim(coefficients, lax.axis_index("field") * row_count, row_count, 0)
    own = jnp.pad(own, ((0, height - row_count), (0, 0)))
    moved = newton_rows(snaps, total, everyone, counts, own, snap_coef)
    owner_row = jnp.pad(
        owners.reshape(devices, row_count), ((0, 0), (0, height - row_count)), constant_values=-1.0
    ).reshape(1, devices * height)
    slots = 2 * block_rows // dom_size
    placed = place_rows(moved, owner_row, slots)
    return placed.reshape(1, dom_size, slots, rank)


def solution(mesh):
    return jax.shard_map(
        body,
        mesh=mesh,
        in_specs=(
            P("dom", None),
            P("dom"),
            P("dom", None),
            P(),
            P(("field", "dom"), None),
            P(("field", "dom")),
            P(("field", "dom")),
        ),
        out_specs=P("dom", None, None, None),
        check_vma=False,
    )
```

time: 496 us -> 196 us (0.40)
  other arithmetic: 176 us -> 4.1 us
  waiting for transfers between devices: 121 us -> 0 us
  Pallas kernels: 121 us -> 184 us
  blocking collectives: 52 us -> 0 us
  between operations: 14.9 us -> 0.07 us
  matrix products: 5.68 us -> 0 us
    another operation x8 -> x4, other arithmetic: 173 us -> 0.68 us  [the longest x2 0.67 us: body(): jnp.stack([copies.astype(jnp.float32), owner[:, 0].astype(jnp.float32)])]
    psum x1 -> x0, waiting for transfers between devices: 121 us -> none  [body(): sums = lax.psum(sums, ('field', 'dom'))]
    pallas_call x0 -> x4, Pallas kernels: none -> 62.8 us  [the longest x1 26.3 us: reduce_all(): pl.pallas_call(functools.partial(reduce_kernel, half_dom, peers), out_sha...]
    all_gather x2 -> x0, blocking collectives: 37.5 us -> none  [the longest x1 30.6 us: body(): updated = lax.all_gather(updated, 'field', axis=0, tiled=True)]
    unnamed x1 -> x0, blocking collectives: 7.83 us -> none
    all_to_all x1 -> x0, blocking collectives: 6.68 us -> none  [body(): lax.all_to_all(packed, 'dom', split_axis=0, concat_axis=0, tiled=True)]
  transfers between devices with their start and end apart: 1 -> 0, of which waited for: 1 -> 0; matrix products, arithmetic and copies ran while one was open for 0% -> 0% of each run, Pallas kernels for 0% -> 0%
where the time goes in v1:
time: 196 us; the launch traced here: 195 us
  Pallas kernels  184 us (94%)
  local copies, waits for them, and re-layouts  6.91 us (4%)
  other arithmetic  4.1 us (2%)
    pallas_call x1, Pallas kernels, local_sums(): pl.pallas_call(functools.partial(local_kernel, density, snaps), grid=(poi...  121 us
    pallas_call x1, Pallas kernels, reduce_all(): pl.pallas_call(functools.partial(reduce_kernel, half_dom, peers), out_sha...  26.3 us
    pallas_call x1, Pallas kernels, newton_rows(): pl.pallas_call(functools.partial(newton_kernel, snaps), out_shape=jax.Sha...  16.7 us
    pallas_call x1, Pallas kernels, place_rows(): pl.pallas_call(functools.partial(place_kernel, field_size, peers, slots),...  13 us
    pallas_call x1, Pallas kernels, gather_dom(): pl.pallas_call(functools.partial(gather_kernel, dom_size), out_shape=jax....  6.83 us

profile of v1, /device:TPU:0, one launch (start us, length us, event | category | flops | bytes accessed | tf_op | source)
XLA Modules:
  0.0 195.1 jit_solution(5346273529909335929)
XLA Ops:
  0.0 0.7 convert_bitcast_fusion.1
  0.7 0.7 convert_bitcast_fusion
  1.3 0.7 compare_select_fusion
  2.0 0.1 pad.7.clone
  2.1 0.7 constant_dynamic-slice_fusion.own_ref
  2.8 1.4 pad_maximum_fusion.msg_ref
  4.2 6.8 %shard_map.73 = f32[4,72,128]{2,1,0:T(8,128)} custom-call(f32[72,128]{1,0:T(8,128)} %pad_maximum_fusion.msg_ref), custom_call_target="tpu_custom_call" | custom-call | tf_op jit(solution)/shard_map/pallas_call | solution.py:51
  11.0 0.8 slice_reduce_fusion
  11.8 0.9 slice.9
  12.7 0.6 gather_fusion
  13.3 0.6 reshape.38.owner_ref
  13.9 0.1 reshape_squeeze.4.counts_ref
  14.0 0.7 maximum_maximum_fusion.coef_ref
  14.7 121.2 %shard_map.74 = f32[1280,128]{1,0:T(8,128)} custom-call(bf16[272,128]{1,0:T(8,128)(2,1)} %maximum_maximum_fusion.coef_ref, bf16[131072,128]{1,0:T(8,128)(2,1)} %basis_ref.1, f32[1,131072]{1,0:T(1,128)} %bitcast.15, f32[1,131072]{1,0:T(1,128)} %bitcast.16), custom_call_target="tpu_custom_call" | custom-call | tf_op jit(solution)/shard_map/pallas_call | solution.py:95
  136.0 26.3 %shard_map.75 = f32[2,16,40,128]{3,2,1,0:T(8,128)} custom-call(f32[2,16,40,128]{3,2,1,0:T(8,128)} %bitcast.14), custom_call_target="tpu_custom_call" | custom-call | tf_op jit(solution)/shard_map/pallas_call | solution.py:240
  162.3 0.0 copy-start
  162.3 1.1 copy-done
  163.4 16.7 %shard_map.76.moved_ref = f32[8,128]{1,0:T(8,128)S(1)} custom-call(f32[1280,128]{1,0:T(8,128)S(1)} %bitcast.11, f32[256,128]{1,0:T(8,128)S(1)} %bitcast.13, f32[1,256]{1,0:T(1,128)S(1)} %reshape_squeeze.4.counts_ref, f32[8,128]{1,0:T(8,128)S(1)} %constant_dynamic-slice_fusion.own_ref, f32[8,128]{1,0:T(8,128)S(1)} %gather_fusion), custom_call_target="tpu_custom_call" | custom-call | tf_op jit(solution)/shard_map/pallas_call | solution.py:355
  180.1 0.0 copy-start.1
  180.1 0.6 copy-done.1
  180.7 13.0 %shard_map.77 = f32[128,128]{1,0:T(8,128)} custom-call(f32[8,128]{1,0:T(8,128)} %copy-done.1, f32[1,256]{1,0:T(1,128)} %reshape.38.owner_ref), custom_call_target="tpu_custom_call" | custom-call | tf_op jit(solution)/shard_map/pallas_call | solution.py:423
  193.7 1.5 copy.9
  (5 shorter events, 0.0 us)
Async XLA Ops:
  162.3 1.1 copy-start
  180.1 0.6 copy-start.1

commit v2 on v1

--- a/solution.py
+++ b/solution.py
@@ -13,6 +13,7 @@
 MESH = pl.DeviceIdType.MESH
 VMEM = pltpu.MemorySpace.VMEM
 GROUP = 8
+TILE, RING = 8192, 8
 
 
 def round_up(value, unit):
@@ -104,6 +105,136 @@
         out_specs=pl.BlockSpec((padded, rank), lambda i: (0, 0)),
         out_shape=jax.ShapeDtypeStruct((padded, rank), jnp.float32),
         scratch_shapes=[pltpu.VMEM((total, tile), jnp.bfloat16)],
+        compiler_params=pltpu.CompilerParams(
+            dimension_semantics=("arbitrary",), vmem_limit_bytes=56 * 1024 * 1024
+        ),
+    )(stacked, basis, observed.reshape(1, points), precision.reshape(1, points))
+
+
+CHUNK = 256
+PIECE = 64
+
+
+def held_kernel(density, snaps, ring, coef_ref, basis_ref, obs_ref, prec_ref, out_ref, lhs_ref, wide_ref, side_ref):
+    tile, rank = basis_ref.shape
+    particles = coef_ref.shape[0] - 16
+    pieces = particles // PIECE
+    split = particles + snaps // 2 * rank
+    chunks = tile // CHUNK
+    f32 = jnp.float32
+    push, multiply, pop = pltpu.matmul_push_rhs, pltpu.matmul_acc_lhs, pltpu.matmul_pop
+
+    def run(tails, fields, first_a, second_a, first_b, second_b):
+        @pl.when(pl.program_id(0) == 0)
+        def _():
+            out_ref[...] = jnp.zeros_like(out_ref)
+            side_ref[...] = jnp.zeros_like(side_ref)
+            wide_ref[...] = jnp.zeros_like(wide_ref)
+            for ref in [*tails, *fields, first_a, second_a, first_b, second_b]:
+                pop(ref)
+
+        def slot(c):
+            return slice(c % ring * CHUNK, (c % ring + 1) * CHUNK)
+
+        def prepare(c):
+            points, held, turn = slice(c * CHUNK, (c + 1) * CHUNK), slot(c), c % 2
+            basis = basis_ref[points, :]
+            wide_ref[held, :rank] = basis
+            push(wide_ref[held, :], staging_register=turn, mxu_index=0, transpose=True)
+            turned = basis.T
+            multiply(tails[turn], coef_ref[particles:, :], load_staged_rhs=turn)
+            for q in range(pieces):
+                multiply(fields[turn * pieces + q], coef_ref[q * PIECE:(q + 1) * PIECE, :])
+            observed = obs_ref[:, points]
+            weight = density * prec_ref[:, points]
+            slopes = jnp.tanh(pop(tails[turn])[:snaps] - observed)
+            bend = weight * (1.0 - slopes * slopes)
+            for s in range(snaps):
+                start = particles + s * rank
+                lhs_ref[start:start + rank, held] = bend[s:s + 1].astype(jnp.bfloat16) * turned
+            for q in range(pieces):
+                slopes = jnp.tanh(pop(fields[turn * pieces + q]) - observed)
+                lhs_ref[q * PIECE:(q + 1) * PIECE, held] = (weight * slopes).astype(jnp.bfloat16)
+            return turned
+
+        def consume(c, turned):
+            held = slot(c)
+            one = c % 2
+            two = 1 - one
+            wide = wide_ref[held, :]
+            if c + 1 >= chunks:
+                one, two = two, one
+            push(wide, staging_register=one, mxu_index=0)
+            push(wide, staging_register=0, mxu_index=1)
+            multiply(first_a, lhs_ref[:particles, held], load_staged_rhs=one)
+            multiply(second_a, lhs_ref[particles:split, held], load_staged_rhs=0)
+            push(lhs_ref[split:split + CHUNK, held], staging_register=two, mxu_index=0, transpose=True)
+            push(lhs_ref[split + CHUNK:, held], staging_register=1, mxu_index=1, transpose=True)
+            multiply(first_b, turned, load_staged_rhs=two)
+            multiply(second_b, turned, load_staged_rhs=1)
+
+        turned = prepare(0)
+        for c in range(chunks):
+            after = prepare(c + 1) if c + 1 < chunks else None
+            consume(c, turned)
+            turned = after
+        out_ref[:particles, :] += pop(first_a)[:, :rank]
+        out_ref[particles:split, :] += pop(second_a)[:, :rank]
+        side_ref[:, :CHUNK] += pop(first_b)
+        side_ref[:, CHUNK:] += pop(second_b)
+
+        @pl.when(pl.program_id(0) == pl.num_programs(0) - 1)
+        def _():
+            for t in range(2 * CHUNK // rank):
+                start = split + t * rank
+                out_ref[start:start + rank, :] = side_ref[:, t * rank:(t + 1) * rank].T
+
+    unit0, unit1 = pltpu.ACC(0), pltpu.ACC(1)
+    pl.run_scoped(
+        run,
+        [unit0((16, CHUNK), f32)] * 2,
+        [unit0((PIECE, CHUNK), f32)] * (2 * pieces),
+        unit0((particles, CHUNK), f32),
+        unit1((split - particles, CHUNK), f32),
+        unit0((rank, CHUNK), f32),
+        unit1((rank, CHUNK), f32),
+    )
+
+
+def held_fits(particles, snaps, rank, points):
+    entries0 = 2 * (particles + 16) + particles + rank
+    entries1 = snaps // 2 * rank + rank
+    return (
+        2 * rank == CHUNK
+        and snaps * rank == 4 * CHUNK
+        and particles % PIECE == 0
+        and max(entries0, entries1) <= 1024
+        and points % CHUNK == 0
+    )
+
+
+def held_sums(density, stacked, snaps, basis, observed, precision, tile, ring, padded):
+    points, rank = basis.shape
+    particles = stacked.shape[0] - 16
+    tile = math.gcd(points, tile)
+    total = particles + snaps * rank
+    stacked = jnp.concatenate([stacked, jnp.zeros_like(stacked)], axis=1)
+    return pl.pallas_call(
+        functools.partial(held_kernel, density, snaps, ring),
+        grid=(points // tile,),
+        in_specs=[
+            pl.BlockSpec((particles + 16, 2 * rank), lambda i: (0, 0)),
+            pl.BlockSpec((tile, rank), lambda i: (i, 0)),
+            pl.BlockSpec((1, tile), lambda i: (0, i)),
+            pl.BlockSpec((1, tile), lambda i: (0, i)),
+        ],
+        out_specs=pl.BlockSpec((padded, rank), lambda i: (0, 0)),
+        out_shape=jax.ShapeDtypeStruct((padded, rank), jnp.float32),
+        scratch_shapes=[
+            pltpu.VMEM((total, ring * CHUNK), jnp.bfloat16),
+            pltpu.VMEM((ring * CHUNK, 2 * rank), jnp.bfloat16),
+            pltpu.VMEM((rank, 2 * CHUNK), jnp.float32),
+        ],
         compiler_params=pltpu.CompilerParams(
             dimension_semantics=("arbitrary",), vmem_limit_bytes=56 * 1024 * 1024
         ),
@@ -452,7 +583,10 @@
     spare = jnp.zeros((16 - snaps, rank), jnp.float32)
     stacked = jnp.concatenate([everyone, snap_coef, spare], axis=0).astype(jnp.bfloat16)
     padded = round_up(-(-(particles + snaps * rank) // devices), 8) * devices
-    part = local_sums(density, stacked, snaps, basis, observed, precision, 2048, padded)
+    if held_fits(particles, snaps, rank, basis.shape[0]):
+        part = held_sums(density, stacked, snaps, basis, observed, precision, TILE, RING, padded)
+    else:
+        part = local_sums(density, stacked, snaps, basis, observed, precision, 4096, padded)
     total = reduce_all(part)
     row_count = block_rows // field_size
     height = round_up(row_count, 8)

time: 196 us -> 174 us (0.89)
  Pallas kernels: 184 us -> 163 us
    pallas_call x1, Pallas kernels: 121 us -> 99.6 us  [held_sums(): pl.pallas_call(functools.partial(held_kernel, density, snaps, ring), grid...]
where the time goes in v2:
time: 174 us
  Pallas kernels  163 us (94%)
  local copies, waits for them, and re-layouts  7.58 us (4%)
  other arithmetic  3.47 us (2%)
    pallas_call x1, Pallas kernels, held_sums(): pl.pallas_call(functools.partial(held_kernel, density, snaps, ring), grid...  99.6 us
    pallas_call x1, Pallas kernels, reduce_all(): pl.pallas_call(functools.partial(reduce_kernel, half_dom, peers), out_sha...  26.5 us
    pallas_call x1, Pallas kernels, newton_rows(): pl.pallas_call(functools.partial(newton_kernel, snaps), out_shape=jax.Sha...  16.7 us
    pallas_call x1, Pallas kernels, place_rows(): pl.pallas_call(functools.partial(place_kernel, field_size, peers, slots),...  13 us
    pallas_call x1, Pallas kernels, gather_dom(): pl.pallas_call(functools.partial(gather_kernel, dom_size), out_shape=jax....  6.83 us

profile of v2, /device:TPU:0, one launch (start us, length us, event | category | flops | bytes accessed | tf_op | source)
XLA Modules:
  0.0 173.7 jit_solution(1194593588405093665)
XLA Ops:
  0.0 0.7 convert_bitcast_fusion.1
  0.7 0.7 convert_bitcast_fusion
  1.3 0.7 compare_select_fusion
  2.0 0.1 pad.8.clone
  2.1 0.7 constant_dynamic-slice_fusion.own_ref
  2.8 1.4 pad_maximum_fusion.msg_ref
  4.2 6.8 %shard_map.73 = f32[4,72,128]{2,1,0:T(8,128)} custom-call(f32[72,128]{1,0:T(8,128)} %pad_maximum_fusion.msg_ref), custom_call_target="tpu_custom_call" | custom-call | tf_op jit(solution)/shard_map/pallas_call | solution.py:52
  11.0 0.8 slice_reduce_fusion
  11.8 0.9 slice.9
  12.7 0.6 gather_fusion
  13.3 0.6 reshape.38.owner_ref
  13.9 0.1 reshape_squeeze.4.counts_ref
  14.0 0.1 maximum_maximum_fusion
  14.1 0.7 concatenate.12.coef_ref
  14.8 99.6 %shard_map.74 = f32[1280,128]{1,0:T(8,128)} custom-call(bf16[272,256]{1,0:T(8,128)(2,1)} %concatenate.12.coef_ref, bf16[131072,128]{1,0:T(8,128)(2,1)} %basis_ref.1, f32[1,131072]{1,0:T(1,128)} %bitcast.15, f32[1,131072]{1,0:T(1,128)} %bitcast.16), custom_call_target="tpu_custom_call" | custom-call | tf_op jit(solution)/shard_map/pallas_call | solution.py:222
  114.3 26.5 %shard_map.75 = f32[2,16,40,128]{3,2,1,0:T(8,128)} custom-call(f32[2,16,40,128]{3,2,1,0:T(8,128)} %bitcast.14), custom_call_target="tpu_custom_call" | custom-call | tf_op jit(solution)/shard_map/pallas_call | solution.py:371
  140.8 0.0 copy-start
  140.8 1.1 copy-done
  141.9 16.7 %shard_map.76.moved_ref = f32[8,128]{1,0:T(8,128)S(1)} custom-call(f32[1280,128]{1,0:T(8,128)S(1)} %bitcast.11, f32[256,128]{1,0:T(8,128)S(1)} %bitcast.13, f32[1,256]{1,0:T(1,128)S(1)} %reshape_squeeze.4.counts_ref, f32[8,128]{1,0:T(8,128)S(1)} %constant_dynamic-slice_fusion.own_ref, f32[8,128]{1,0:T(8,128)S(1)} %gather_fusion), custom_call_target="tpu_custom_call" | custom-call | tf_op jit(solution)/shard_map/pallas_call | solution.py:486
  158.6 0.0 copy-start.1
  158.6 0.6 copy-done.1
  159.2 13.0 %shard_map.77 = f32[128,128]{1,0:T(8,128)} custom-call(f32[8,128]{1,0:T(8,128)} %copy-done.1, f32[1,256]{1,0:T(1,128)} %reshape.38.owner_ref), custom_call_target="tpu_custom_call" | custom-call | tf_op jit(solution)/shard_map/pallas_call | solution.py:554
  172.2 1.5 copy.9
  (5 shorter events, 0.0 us)
Async XLA Ops:
  140.8 1.1 copy-start
  158.6 0.6 copy-start.1
